TPU v7x, 32 devices: a whole 2x2x4 slice. The times are simulated.
32 devices in a mesh: ctx: 8 (over y, x, core), fsdp: 4 (over z).
Axes of the slice: x: 2, y: 2, z: 4, core: 2. Of those that a mesh axis runs over, the one named last changes fastest.
Arguments:
- tokens: bfloat16 [4096, 1600], P(('fsdp', 'ctx')), may hold values from -6 to 6
- block_table: int32 [8, 2], replicated, may hold values from 0 to 15, as said below
- ln1_gain: bfloat16 [1600], P('fsdp'), may hold values from 0.099609375 to 1.8984375
- ln1_bias: bfloat16 [1600], P('fsdp'), may hold values from -1.75 to 1.75
- qkv_weight: bfloat16 [1600, 4800], P('fsdp'), may hold values from -0.15625 to 0.15625
- query_bias: bfloat16 [1600], P('fsdp'), may hold values from -3 to 3
- value_bias: bfloat16 [1600], P('fsdp'), may hold values from -0.875 to 0.875
- proj_weight: bfloat16 [1600, 1600], P('fsdp'), may hold values from -1.25 to 1.25
- proj_bias: bfloat16 [1600], P('fsdp'), may hold values from -1.75 to 1.75
- ln2_gain: bfloat16 [1600], P('fsdp'), may hold values from 0.099609375 to 1.8984375
- ln2_bias: bfloat16 [1600], P('fsdp'), may hold values from -1.75 to 1.75
- fc_weight: bfloat16 [1600, 6400], P('fsdp'), may hold values from -0.15625 to 0.15625
- fc_bias: bfloat16 [6400], P('fsdp'), may hold values from -3 to 3
- out_weight: bfloat16 [6400, 1600], P('fsdp'), may hold values from -0.078125 to 0.078125
- out_bias: bfloat16 [1600], P('fsdp'), may hold values from -1.75 to 1.75
- cotangent: bfloat16 [4096, 1600], P(('fsdp', 'ctx')), may hold values from -6 to 6
Outputs:
- layer_out: bfloat16 [4096, 1600], P(('fsdp', 'ctx'))
- grad_tokens: bfloat16 [4096, 1600], P(('fsdp', 'ctx'))
- grad_ln1_gain: float32 [1600], P('fsdp')
- grad_ln1_bias: float32 [1600], P('fsdp')
- grad_qkv_weight: float32 [1600, 4800], P('fsdp')
- grad_query_bias: float32 [1600], P('fsdp')
- grad_value_bias: float32 [1600], P('fsdp')
- grad_proj_weight: float32 [1600, 1600], P('fsdp')
- grad_proj_bias: float32 [1600], P('fsdp')
- grad_ln2_gain: float32 [1600], P('fsdp')
- grad_ln2_bias: float32 [1600], P('fsdp')
- grad_fc_weight: float32 [1600, 6400], P('fsdp')
- grad_fc_bias: float32 [6400], P('fsdp')
- grad_out_weight: float32 [6400, 1600], P('fsdp')
- grad_out_bias: float32 [1600], P('fsdp')
Inputs may be any that keep to these rules, and one draw needn't show every extreme that they name: `block_table`: row i is (p_i, 15 - p_i) with p_i below 8; every block number appears exactly once.
All inputs are finite; a program needn't handle non-finite values.
Results may differ from a plain program's by a relative error of at most 0.02.
Values may be sent and summed in bfloat16 or wider, within the bound.
A program may use at most 256 MiB of HBM per device.

v0:
```python
import math
import jax
import jax.numpy as jnp
from jax import lax
from jax.sharding import PartitionSpec as P

HEADS = 25


def layer_norm(values, gain_vec, shift_vec):
    centre = values - jnp.mean(values, axis=-1, keepdims=True)
    spread = jnp.mean(centre * centre, axis=-1, keepdims=True)
    return centre * lax.rsqrt(spread + 1e-05) * gain_vec + shift_vec


def gelu_tanh(values):
    return jax.nn.gelu(values, approximate=True)


def body(
    tokens,
    block_table,
    ln1_gain,
    ln1_bias,
    qkv_weight,
    query_bias,
    value_bias,
    proj_weight,
    proj_bias,
    ln2_gain,
    ln2_bias,
    fc_weight,
    fc_bias,
    out_weight,
    out_bias,
    cotangent,
):
    row_count = tokens.shape[0]
    model_width = tokens.shape[1]
    block_rows = row_count // 2
    head_dim = model_width // HEADS
    score_scale = head_dim ** (-0.5)
    ctx_index = lax.axis_index("ctx")
    own_blocks = lax.dynamic_slice_in_dim(block_table, ctx_index, 1, 0).reshape(-1)
    offsets = jnp.arange(block_rows, dtype=jnp.int32)
    query_pos = (own_blocks[:, None] * block_rows + offsets[None, :]).reshape(-1)
    key_pos = (block_table.reshape(-1)[:, None] * block_rows + offsets[None, :]).reshape(-1)
    seq_len = key_pos.shape[0]
    key_block = math.gcd(seq_len, 512)
    block_count = seq_len // key_block
    pos_blocks = key_pos.reshape(block_count, key_block)
    gain_one, shift_one, qkv_full, q_bias, v_bias, proj_full, proj_b = (
        lax.all_gather(ln1_gain, "fsdp", axis=0, tiled=True),
        lax.all_gather(ln1_bias, "fsdp", axis=0, tiled=True),
        lax.all_gather(qkv_weight, "fsdp", axis=0, tiled=True),
        lax.all_gather(query_bias, "fsdp", axis=0, tiled=True),
        lax.all_gather(value_bias, "fsdp", axis=0, tiled=True),
        lax.all_gather(proj_weight, "fsdp", axis=0, tiled=True),
        lax.all_gather(proj_bias, "fsdp", axis=0, tiled=True),
    )
    inputs = tokens.astype(jnp.float32)
    gain_one_f = gain_one.astype(jnp.float32)
    shift_one_f = shift_one.astype(jnp.float32)
    normed_one = layer_norm(inputs, gain_one_f, shift_one_f).astype(jnp.bfloat16)
    bias_row = jnp.concatenate([q_bias, jnp.zeros_like(q_bias), v_bias]).astype(jnp.float32)
    joined = jnp.dot(normed_one, qkv_full, preferred_element_type=jnp.float32) + bias_row
    query_rows = joined[:, :model_width].astype(jnp.bfloat16).reshape(row_count, HEADS, head_dim)
    key_local = joined[:, model_width : 2 * model_width].astype(jnp.bfloat16)
    value_local = joined[:, 2 * model_width :].astype(jnp.bfloat16)
    key_all, value_all = (
        lax.all_gather(key_local, "ctx", axis=0, tiled=True),
        lax.all_gather(value_local, "ctx", axis=0, tiled=True),
    )

    def scores_of(key_tile, pos_tile):
        raw_scores = jnp.einsum(
            "qhd,khd->hqk", query_rows, key_tile, preferred_element_type=jnp.float32
        )
        allowed = pos_tile[None, :] <= query_pos[:, None]
        return (jnp.where(allowed[None], raw_scores * score_scale, -1e30), allowed)

    key_tiles = key_all.reshape(block_count, key_block, HEADS, head_dim)
    value_tiles = value_all.reshape(block_count, key_block, HEADS, head_dim)

    def stat_step(carried, tile_set):
        top_prev, total_prev = carried
        scores, allowed = scores_of(tile_set[0], tile_set[1])
        top_new = jnp.maximum(top_prev, jnp.max(scores, axis=-1))
        total_new = total_prev * jnp.exp(top_prev - top_new) + jnp.sum(
            jnp.exp(scores - top_new[..., None]), axis=-1
        )
        return ((top_new, total_new), None)

    start_stats = (
        jnp.full((HEADS, row_count), -1e30, jnp.float32),
        jnp.zeros((HEADS, row_count), jnp.float32),
    )
    (top_all, total_all), _ = lax.scan(stat_step, start_stats, (key_tiles, pos_blocks))
    log_total = top_all + jnp.log(total_all)

    def out_step(summed, tile_set):
        scores, allowed = scores_of(tile_set[0], tile_set[2])
        soft_w = jnp.exp(scores - log_total[..., None]).astype(jnp.bfloat16)
        return (
            summed
            + jnp.einsum("hqk,khd->qhd", soft_w, tile_set[1], preferred_element_type=jnp.float32),
            None,
        )

    heads_f, _ = lax.scan(
        out_step,
        jnp.zeros((row_count, HEADS, head_dim), jnp.float32),
        (key_tiles, value_tiles, pos_blocks),
    )
    heads_low = heads_f.reshape(row_count, model_width).astype(jnp.bfloat16)
    middle = (
        inputs
        + jnp.dot(heads_low, proj_full, preferred_element_type=jnp.float32)
        + proj_b.astype(jnp.float32)
    )
    fsdp_count = lax.axis_size("fsdp")
    width_share = model_width // fsdp_count
    small_stack = jnp.stack([ln2_gain, ln2_bias, out_bias], axis=1)
    small_tiled = jnp.tile(small_stack, (1, fsdp_count))
    fc_cols, small_full = (
        lax.all_to_all(fc_weight, "fsdp", split_axis=1, concat_axis=0, tiled=True),
        lax.all_to_all(small_tiled, "fsdp", split_axis=1, concat_axis=0, tiled=True),
    )
    gain_two_f = small_full[:, 0].astype(jnp.float32)
    shift_two_f = small_full[:, 1].astype(jnp.float32)
    out_b_f = small_full[:, 2].astype(jnp.float32)
    normed_two = layer_norm(middle, gain_two_f, shift_two_f).astype(jnp.bfloat16)
    group_normed, group_upstream = (
        lax.all_gather(normed_two, "fsdp", axis=0, tiled=True),
        lax.all_gather(cotangent, "fsdp", axis=0, tiled=True),
    )
    hidden_pre = jnp.dot(
        group_normed, fc_cols, preferred_element_type=jnp.float32
    ) + fc_bias.astype(jnp.float32)
    hidden = gelu_tanh(hidden_pre).astype(jnp.bfloat16)
    rows = hidden
    summed_out = lax.psum_scatter(
        jnp.dot(rows, out_weight, preferred_element_type=jnp.float32).astype(jnp.bfloat16),
        "fsdp",
        scatter_dimension=0,
        tiled=True,
    ).astype(jnp.float32)
    output = middle + summed_out + out_b_f
    out_rows = output.astype(jnp.bfloat16)
    owned_ow = jnp.einsum("tf,td->fd", hidden, group_upstream, preferred_element_type=jnp.float32)
    full_out_b = jnp.sum(group_upstream.astype(jnp.float32), axis=0)
    owned_ob = lax.dynamic_slice_in_dim(
        full_out_b, lax.axis_index("fsdp") * width_share, width_share, 0
    )
    grad_hidden = jnp.einsum(
        "td,fd->tf", group_upstream, out_weight, preferred_element_type=jnp.float32
    )
    _, gelu_pull = jax.vjp(gelu_tanh, hidden_pre)
    grad_pre = gelu_pull(grad_hidden)[0].astype(jnp.bfloat16)
    grad_fc_cols = jnp.einsum(
        "tc,tf->cf", group_normed, grad_pre, preferred_element_type=jnp.float32
    )
    owned_fcb = jnp.sum(grad_pre.astype(jnp.float32), axis=0)
    rows = grad_pre
    grad_normed_two = lax.psum_scatter(
        jnp.einsum("tf,cf->tc", rows, fc_cols, preferred_element_type=jnp.float32).astype(
            jnp.bfloat16
        ),
        "fsdp",
        scatter_dimension=0,
        tiled=True,
    ).astype(jnp.float32)
    _, norm_pull_two = jax.vjp(layer_norm, middle, gain_two_f, shift_two_f)
    grad_mid_norm, grad_gain_two, grad_shift_two = norm_pull_two(grad_normed_two)
    grad_middle = cotangent.astype(jnp.float32) + grad_mid_norm
    norm_pair = jnp.stack([grad_gain_two, grad_shift_two], axis=1)
    owned_fcw, norm_parts = (
        lax.all_to_all(
            grad_fc_cols.astype(jnp.bfloat16), "fsdp", split_axis=0, concat_axis=1, tiled=True
        ).astype(grad_fc_cols.dtype),
        lax.all_to_all(
            norm_pair.astype(jnp.bfloat16), "fsdp", split_axis=0, concat_axis=1, tiled=True
        ).astype(norm_pair.dtype),
    )
    norm_sums = jnp.sum(norm_parts.reshape(width_share, fsdp_count, 2), axis=1)
    owned_g2 = norm_sums[:, 0]
    owned_b2 = norm_sums[:, 1]
    total_g2, total_b2, total_fcw, total_fcb, total_ow, total_ob = (
        lax.psum(owned_g2.astype(jnp.bfloat16), "ctx").astype(jnp.float32),
        lax.psum(owned_b2.astype(jnp.bfloat16), "ctx").astype(jnp.float32),
        lax.psum(owned_fcw.astype(jnp.bfloat16), "ctx").astype(jnp.float32),
        lax.psum(owned_fcb.astype(jnp.bfloat16), "ctx").astype(jnp.float32),
        lax.psum(owned_ow.astype(jnp.bfloat16), "ctx").astype(jnp.float32),
        lax.psum(owned_ob.astype(jnp.bfloat16), "ctx").astype(jnp.float32),
    )
    grad_branch = grad_middle.astype(jnp.bfloat16)
    grad_proj_w = jnp.einsum(
        "tc,td->cd", heads_low, grad_branch, preferred_element_type=jnp.float32
    )
    grad_proj_b = jnp.sum(grad_branch.astype(jnp.float32), axis=0)
    grad_heads = jnp.einsum(
        "td,cd->tc", grad_branch, proj_full, preferred_element_type=jnp.float32
    ).astype(jnp.bfloat16)
    grad_heads_split = grad_heads.reshape(row_count, HEADS, head_dim)
    delta_rows = jnp.sum(grad_heads_split.astype(jnp.float32) * heads_f, axis=-1).T

    def grad_step(grad_query, tile_set):
        key_tile, value_tile, pos_tile = tile_set
        scores, allowed = scores_of(key_tile, pos_tile)
        soft_w = jnp.exp(scores - log_total[..., None])
        grad_soft = jnp.einsum(
            "qhd,khd->hqk", grad_heads_split, value_tile, preferred_element_type=jnp.float32
        )
        grad_raw = jnp.where(
            allowed[None], soft_w * (grad_soft - delta_rows[..., None]) * score_scale, 0.0
        ).astype(jnp.bfloat16)
        grad_query = grad_query + jnp.einsum(
            "hqk,khd->qhd", grad_raw, key_tile, preferred_element_type=jnp.float32
        )
        grad_key = jnp.einsum(
            "hqk,qhd->khd", grad_raw, query_rows, preferred_element_type=jnp.float32
        )
        grad_value = jnp.einsum(
            "hqk,qhd->khd",
            soft_w.astype(jnp.bfloat16),
            grad_heads_split,
            preferred_element_type=jnp.float32,
        )
        return (grad_query, (grad_key, grad_value))

    grad_query, (key_grads, value_grads) = lax.scan(
        grad_step,
        jnp.zeros((row_count, HEADS, head_dim), jnp.float32),
        (key_tiles, value_tiles, pos_blocks),
    )
    key_terms = key_grads.reshape(seq_len, model_width)
    value_terms = value_grads.reshape(seq_len, model_width)
    key_mine, value_mine = (
        lax.psum_scatter(
            key_terms.astype(jnp.bfloat16), "ctx", scatter_dimension=0, tiled=True
        ).astype(jnp.float32),
        lax.psum_scatter(
            value_terms.astype(jnp.bfloat16), "ctx", scatter_dimension=0, tiled=True
        ).astype(jnp.float32),
    )
    grad_joined = jnp.concatenate(
        [grad_query.reshape(row_count, model_width), key_mine, value_mine], axis=1
    ).astype(jnp.bfloat16)
    grad_q_bias = jnp.sum(grad_joined[:, :model_width].astype(jnp.float32), axis=0)
    grad_v_bias = jnp.sum(grad_joined[:, 2 * model_width :].astype(jnp.float32), axis=0)
    grad_qkv_w = jnp.einsum(
        "tc,tk->ck", normed_one, grad_joined, preferred_element_type=jnp.float32
    )
    grad_normed_one = jnp.einsum(
        "tk,ck->tc", grad_joined, qkv_full, preferred_element_type=jnp.float32
    )
    _, norm_pull_one = jax.vjp(layer_norm, inputs, gain_one_f, shift_one_f)
    grad_in_norm, grad_gain_one, grad_shift_one = norm_pull_one(grad_normed_one)
    grad_inputs = (grad_middle + grad_in_norm).astype(jnp.bfloat16)
    owned_g1, owned_b1, owned_qkv, owned_qb, owned_vb, owned_pw, owned_pb = (
        lax.psum_scatter(
            grad_gain_one.astype(jnp.bfloat16), "fsdp", scatter_dimension=0, tiled=True
        ).astype(jnp.float32),
        lax.psum_scatter(
            grad_shift_one.astype(jnp.bfloat16), "fsdp", scatter_dimension=0, tiled=True
        ).astype(jnp.float32),
        lax.psum_scatter(
            grad_qkv_w.astype(jnp.bfloat16), "fsdp", scatter_dimension=0, tiled=True
        ).astype(jnp.float32),
        lax.psum_scatter(
            grad_q_bias.astype(jnp.bfloat16), "fsdp", scatter_dimension=0, tiled=True
        ).astype(jnp.float32),
        lax.psum_scatter(
            grad_v_bias.astype(jnp.bfloat16), "fsdp", scatter_dimension=0, tiled=True
        ).astype(jnp.float32),
        lax.psum_scatter(
            grad_proj_w.astype(jnp.bfloat16), "fsdp", scatter_dimension=0, tiled=True
        ).astype(jnp.float32),
        lax.psum_scatter(
            grad_proj_b.astype(jnp.bfloat16), "fsdp", scatter_dimension=0, tiled=True
        ).astype(jnp.float32),
    )
    total_g1, total_b1, total_qkv, total_qb, total_vb, total_pw, total_pb = (
        lax.psum(owned_g1.astype(jnp.bfloat16), "ctx").astype(jnp.float32),
        lax.psum(owned_b1.astype(jnp.bfloat16), "ctx").astype(jnp.float32),
        lax.psum(owned_qkv.astype(jnp.bfloat16), "ctx").astype(jnp.float32),
        lax.psum(owned_qb.astype(jnp.bfloat16), "ctx").astype(jnp.float32),
        lax.psum(owned_vb.astype(jnp.bfloat16), "ctx").astype(jnp.float32),
        lax.psum(owned_pw.astype(jnp.bfloat16), "ctx").astype(jnp.float32),
        lax.psum(owned_pb.astype(jnp.bfloat16), "ctx").astype(jnp.float32),
    )
    return (
        out_rows,
        grad_inputs,
        total_g1,
        total_b1,
        total_qkv,
        total_qb,
        total_vb,
        total_pw,
        total_pb,
        total_g2,
        total_b2,
        total_fcw,
        total_fcb,
        total_ow,
        total_ob,
    )


def solution(mesh):
    placed = (
        P(("fsdp", "ctx"), None),
        P(),
        P("fsdp"),
        P("fsdp"),
        P("fsdp", None),
        P("fsdp"),
        P("fsdp"),
        P("fsdp", None),
        P("fsdp"),
        P("fsdp"),
        P("fsdp"),
        P("fsdp", None),
        P("fsdp"),
        P("fsdp", None),
        P("fsdp"),
        P(("fsdp", "ctx"), None),
    )
    return jax.shard_map(
        body,
        mesh=mesh,
        in_specs=placed,
        out_specs=(
            P(("fsdp", "ctx"), None),
            P(("fsdp", "ctx"), None),
            P("fsdp"),
            P("fsdp"),
            P("fsdp", None),
            P("fsdp"),
            P("fsdp"),
            P("fsdp", None),
            P("fsdp"),
            P("fsdp"),
            P("fsdp"),
            P("fsdp", None),
            P("fsdp"),
            P("fsdp", None),
            P("fsdp"),
        ),
        check_vma=False,
    )
```

profile of v0, /device:TPU:0, one launch (start us, length us, event | category | flops | bytes accessed | tf_op | source)
XLA Modules:
  0.0 1569.6 jit_solution(5104515425968146760)
XLA Ops:
  10.6 21.1 %all-reduce.13 = (bf16[1600]{0:T(1024)(128)(2,1)S(1)}, bf16[1600]{0:T(1024)(128)(2,1)S(1)}, bf16[1600]{0:T(1024)(128)(2,1)S(1)}, bf16[1600]{0:T(1024)(128)(2,1)S(1)}, bf16[1600]{0:T(1024)(128)(2,1)S(1)}) all-reduce(bf16[1600]{0:T(1024)(128)(2,1)S(1)} %dynamic-update-slice.2, ...), channel_id=1, replica_groups=mesh['ctx'=8,'fsdp'=4] {'fsdp'}, use_global_device_ids=true, to_apply=%add.2 | all-reduce | flops 8000 | bytes 32000
  32.8 246.5 %all-gather.7.cloned.1.call-done = bf16[1600,4800]{1,0:T(8,128)(2,1)} async-done(((bf16[400,4800]{1,0:T(8,128)(2,1)}), bf16[1600,4800]{1,0:T(8,128)(2,1)}) %all-gather.7.cloned.1.call-update) | async-done | bytes 15360016 | tf_op jit(solution)/shard_map/all_gather | solution.py:55
  279.4 12.1 fusion.80
  299.0 11.7 all_to_all.51
  310.7 5.9 copy.78
  316.8 5.1 all-to-all-start.1
  324.4 8.5 reshape.304
  335.8 19.6 %while.39 = (s32[]{:T(128)}, f32[25,128]{1,0:T(8,128)S(1)}, f32[25,128]{1,0:T(8,128)S(1)}, s32[2,512]{1,0:T(2,128)S(1)}, bf16[2,512,25,64]{1,3,2,0:T(8,128)(2,1)...) while((s32[]{:T(128)}, f32[25,128]{1,0:T(8,128)S(1)}, ...), condition=%wide.region_5.6_spmd.clone, body=%wide.region_2.5_spmd.clone.sunk | while | flops 221265664 | bytes 15526528 | solution.py:98
  336.1 5.2 fusion.175
  345.9 5.2 fusion.175
  355.3 4.9 all-gather.9.cloned.1.call-done
  360.2 8.5 reshape.303
  368.7 4.8 copy.75
  373.5 21.0 %while.40 = (s32[]{:T(128)}, f32[128,25,64]{0,2,1:T(8,128)}, bf16[2,512,25,64]{1,3,2,0:T(8,128)(2,1)}, s32[2,512]{1,0:T(2,128)S(1)}, bf16[2,512,25,64]{1,3,2,0:T...) while((s32[]{:T(128)}, f32[128,25,64]{0,2,1:T(8,128)}, ...), condition=%wide.region_7.8_spmd.clone, body=%wide.region_6.7_spmd.clone.sunk | while | flops 426459264 | bytes 5482114 | solution.py:110
  373.8 4.7 fusion.181
  378.8 5.0 fusion.181
  396.5 129.3 %all-gather.13.cloned.1.call-done = bf16[1600,1600]{1,0:T(8,128)(2,1)} async-done(((bf16[400,1600]{1,0:T(8,128)(2,1)}), bf16[1600,1600]{1,0:T(8,128)(2,1)}) %all-gather.13.cloned.1.call-update) | async-done | bytes 5120016 | tf_op jit(solution)/shard_map/all_gather | solution.py:58
  525.8 5.0 fusion.125
  533.0 31.9 %all-gather.17.cloned.1.call-done = bf16[512,1600]{0,1:T(8,128)(2,1)} async-done(((bf16[128,1600]{0,1:T(8,128)(2,1)}), bf16[512,1600]{0,1:T(8,128)(2,1)}) %all-gather.17.cloned.1.call-update) | async-done | bytes 1638416 | tf_op jit(solution)/shard_map/all_gather | solution.py:135
  564.9 7.9 fusion.126
  572.8 31.1 %all-gather.15.cloned.1.call-done = bf16[512,1600]{0,1:T(8,128)(2,1)} async-done(((bf16[128,1600]{0,1:T(8,128)(2,1)}), bf16[512,1600]{0,1:T(8,128)(2,1)}) %all-gather.15.cloned.1.call-update) | async-done | bytes 1638416 | tf_op jit(solution)/shard_map/all_gather | solution.py:134
  603.9 11.7 fusion.118
  616.8 6.7 convolution_convert_fusion.4
  627.1 35.8 %reduce-scatter.21.cloned.1.call-done = bf16[128,1600]{1,0:T(8,128)(2,1)} async-done(((bf16[512,1600]{1,0:T(8,128)(2,1)}), bf16[128,1600]{1,0:T(8,128)(2,1)}) %reduce-scatter.21.cloned.1.call-update) | async-done | bytes 409616
  675.4 49.1 %while.41 = (s32[]{:T(128)}, f32[128,25,64]{0,2,1:T(8,128)}, bf16[2,512,25,64]{1,3,2,0:T(8,128)(2,1)}, bf16[2,512,25,64]{1,3,2,0:T(8,128)(2,1)}, bf16[2,512,25,6...) while((s32[]{:T(128)}, f32[128,25,64]{0,2,1:T(8,128)}, ...), condition=%wide.region_16.17_spmd.clone, body=%wide.region_15.16_spmd.clone.sunk | while | flops 1068712064 | bytes 150980000 | solution.py:231
  675.8 5.2 fusion.192
  681.3 6.4 fusion.193
  700.1 5.1 fusion.192
  705.5 6.4 fusion.193
  724.5 5.3 copy.82
  750.5 30.1 %reduce-scatter.25.cloned.1.call-done = bf16[128,1600]{1,0:T(8,128)(2,1)} async-done(((bf16[1024,1600]{1,0:T(8,128)(2,1)}), bf16[128,1600]{1,0:T(8,128)(2,1)}) %reduce-scatter.25.cloned.1.call-update) | async-done | bytes 409616
  781.9 50.1 %reduce-scatter.23.cloned.1.call-done = bf16[128,1600]{1,0:T(8,128)(2,1)} async-done(((bf16[1024,1600]{1,0:T(8,128)(2,1)}), bf16[128,1600]{1,0:T(8,128)(2,1)}) %reduce-scatter.23.cloned.1.call-update) | async-done | bytes 409616
  833.4 8.5 convolution_convert_fusion
  843.3 6.3 convolution_convert_fusion.2
  849.6 5.1 all-to-all-start.3
  855.0 8.0 convolution_convert_fusion.5
  866.8 8.1 convolution_convert_fusion.1
  874.9 176.1 %all-to-all-done.3 = bf16[4,400,1600]{2,1,0:T(8,128)(2,1)} async-done(((bf16[4,400,1600]{2,1,0:T(8,128)(2,1)}), bf16[4,400,1600]{2,1,0:T(8,128)(2,1)}, u32[]{:S(2)}, u32[]{:S(2)}) %all-to-all-start.3) | async-done | bytes 5120032 | tf_op jit(solution)/shard_map/all_to_all | solution.py:178
  1051.0 6.9 copy.84
  1057.9 9.8 all_to_all.59
  1067.8 228.2 %reduce-scatter.15.cloned.1.call-done = bf16[400,4800]{1,0:T(8,128)(2,1)} async-done(((bf16[1600,4800]{1,0:T(8,128)(2,1)}), bf16[400,4800]{1,0:T(8,128)(2,1)}) %reduce-scatter.15.cloned.1.call-update) | async-done | bytes 3840016 | tf_op jit(solution)/shard_map/reduce_scatter | solution.py:267
  1301.9 33.4 %reduce-scatter.19.cloned.1.call-done = bf16[128,1600]{1,0:T(8,128)(2,1)} async-done(((bf16[512,1600]{1,0:T(8,128)(2,1)}), bf16[128,1600]{1,0:T(8,128)(2,1)}) %reduce-scatter.19.cloned.1.call-update) | async-done | bytes 409616
  1336.7 9.3 fusion.117
  1346.6 16.9 %all-reduce.12 = (bf16[1600]{0:T(1024)(128)(2,1)S(1)}, bf16[1600]{0:T(1024)(128)(2,1)S(1)}, bf16[1600]{0:T(1024)(128)(2,1)S(1)}, bf16[1600]{0:T(1024)(128)(2,1)S(1)}, bf16[1600]{0:T(1024)(128)(2,1)S(1)}) all-reduce(bf16[1600]{0:T(1024)(128)(2,1)S(1)} %get-tuple-element.374, ...), channel_id=6, replica_groups=mesh['ctx'=8,'fsdp'=4] {'fsdp'}, use_global_device_ids=true, to_apply=%region_22.23.clone | all-reduce | flops 8000 | bytes 32000
  1363.9 24.1 %all-reduce.10 = (bf16[400]{0:T(512)(128)(2,1)S(1)}, bf16[400]{0:T(512)(128)(2,1)S(1)}, bf16[400]{0:T(512)(128)(2,1)S(1)}, bf16[400]{0:T(512)(128)(2,1)S(1)}, bf...) all-reduce(bf16[400]{0:T(512)(128)(2,1)S(1)} %dynamic-slice.6, ...), channel_id=1, replica_groups=mesh['ctx'=8,'fsdp'=4] {'ctx'}, use_global_device_ids=true, to_apply=%region_23.24 | all-reduce | flops 4800 | bytes 19200 | tf_op jit(solution)/shard_map/psum | solution.py:284
  1395.2 150.3 %all-reduce.16.cloned.1.call-done = (bf16[400,4800]{1,0:T(8,128)(2,1)}, bf16[400,1600]{1,0:T(8,128)(2,1)}, bf16[400,6400]{1,0:T(8,128)(2,1)}, bf16[1600,1600]{1,0:T(8,128)(2,1)}) async-done(((bf16[400,4800]{1,0:T(8,128)(2,1)}, bf16[400,1600]{1,0:T(8,128)(2,1)}, bf16[400,6400]{1,0:T(8,128)(2,1)}, bf16[1600,1600]{1,0:T(8,128)(2,1)}), (bf16[400,4800]{1,0:T(8,128)(2,1)}, bf16[400,1600]{1,0:T(8,128)(2,1)}, ...) | async-done | bytes 15360016 | tf_op jit(solution)/shard_map/psum | solution.py:286
  1545.5 6.0 convert_element_type.266
  1557.9 4.8 convert_element_type.281
  (307 shorter events, 122.6 us)
Async XLA Ops:
  7.2 24.6 %copy-start.7 = (bf16[128,1600]{0,1:T(8,128)(2,1)S(1)}, bf16[128,1600]{0,1:T(8,128)(2,1)}, u32[]{:S(2)}) copy-start(bf16[128,1600]{0,1:T(8,128)(2,1)} %param.22) | copy-start | bytes 1228804
  7.3 272.1 %all-gather.7.cloned.1.call-start = ((), (), s32[]{:S(2)}) async-start(), calls=%async_computation.10 | async-start | bytes 19456000 | tf_op jit(solution)/shard_map/all_gather | solution.py:55
  8.0 316.4 %all-gather.11.cloned.1.call-start = ((), (), s32[]{:S(2)}) async-start(), calls=%async_computation.12 | async-start | bytes 3686400 | tf_op jit(solution)/shard_map/all_gather | solution.py:71
  31.7 259.8 %copy-start.28 = (f32[1600]{0:T(1024)}, f32[1600]{0:T(1024)S(1)}, u32[]{:S(2)}) copy-start(f32[1600]{0:T(1024)S(1)} %convert_element_type.230) | copy-start | bytes 19204
  31.8 259.7 %copy-start.30 = (f32[1600]{0:T(1024)}, f32[1600]{0:T(1024)S(1)}, u32[]{:S(2)}) copy-start(f32[1600]{0:T(1024)S(1)} %convert_element_type.231) | copy-start | bytes 19204
  32.1 259.4 %copy-start.33 = (f32[128]{0:T(128)}, f32[128]{0:T(128)S(1)}, u32[]{:S(2)}) copy-start(f32[128]{0:T(128)S(1)} %broadcast_multiply_fusion.2) | copy-start | bytes 1540
  32.8 258.7 %copy-start.35 = (f32[128]{0:T(128)}, f32[128]{0:T(128)S(1)}, u32[]{:S(2)}) copy-start(f32[128]{0:T(128)S(1)} %fusion.110) | copy-start | bytes 1540
  291.6 7.0 copy-start.39
  292.7 67.6 %all-gather.9.cloned.1.call-start = ((), (), s32[]{:S(2)}) async-start(), calls=%async_computation.11 | async-start | bytes 3686400 | tf_op jit(solution)/shard_map/all_gather | solution.py:72
  293.4 232.4 %all-gather.13.cloned.1.call-start = ((), (), s32[]{:S(2)}) async-start(), calls=%async_computation.13 | async-start | bytes 6656000 | tf_op jit(solution)/shard_map/all_gather | solution.py:58
  294.7 22.1 %all-to-all-start = ((bf16[400,4,3]{0,2,1:T(4,128)(2,1)}), bf16[400,4,3]{0,2,1:T(4,128)(2,1)S(1)}, u32[]{:S(2)}, u32[]{:S(2)}) async-start(bf16[400,4,3]{0,2,1:T(4,128)(2,1)} %tile.2), calls=%async_computation | async-start | bytes 32768 | tf_op jit(solution)/shard_map/all_to_all | solution.py:127
  297.9 267.0 %all-gather.17.cloned.1.call-start = ((), (), s32[]{:S(2)}) async-start(), calls=%async_computation.15 | async-start | bytes 2048000 | tf_op jit(solution)/shard_map/all_gather | solution.py:135
  316.8 256.0 %all-to-all-start.1 = ((bf16[400,4,1600]{2,0,1:T(8,128)(2,1)}), bf16[400,4,1600]{2,0,1:T(8,128)(2,1)}, u32[]{:S(2)}, u32[]{:S(2)}) async-start(bf16[400,4,1600]{2,0,1:T(8,128)(2,1)} %copy.78), calls=%async_computation.1 | async-start | bytes 10649600 | tf_op jit(solution)/shard_map/all_to_all | solution.py:126
  321.9 282.0 %all-gather.15.cloned.1.call-start = ((), (), s32[]{:S(2)}) async-start(), calls=%async_computation.14 | async-start | bytes 2048000 | tf_op jit(solution)/shard_map/all_gather | solution.py:134
  525.8 7.2 copy-start.37
  532.9 130.0 %reduce-scatter.21.cloned.1.call-start = ((), (), s32[]{:S(2)}) async-start(), calls=%async_computation.19 | async-start | bytes 2129920
  627.1 153.6 %reduce-scatter.25.cloned.1.call-start = ((), (), s32[]{:S(2)}) async-start(), calls=%async_computation.21 | async-start | bytes 3833856
  675.8 5.2 copy-start
  692.3 6.0 copy-start.13
  700.1 5.2 copy-start
  712.0 4.8 copy-start.15
  716.8 6.0 copy-start.13
  734.3 97.8 %reduce-scatter.23.cloned.1.call-start = ((), (), s32[]{:S(2)}) async-start(), calls=%async_computation.20 | async-start | bytes 3833856
  744.0 323.8 %reduce-scatter.17.cloned.1.call-start = ((), (), s32[]{:S(2)}) async-start(), calls=%async_computation.17 | async-start | bytes 6656000 | tf_op jit(solution)/shard_map/reduce_scatter | solution.py:276
  749.1 84.2 %copy-start.8 = (bf16[128,1600]{0,1:T(8,128)(2,1)S(1)}, bf16[128,1600]{0,1:T(8,128)(2,1)}, u32[]{:S(2)}) copy-start(bf16[128,1600]{0,1:T(8,128)(2,1)} %param.22) | copy-start | bytes 1228804
  749.1 84.2 %copy-start.29 = (f32[1600]{0:T(1024)S(1)}, f32[1600]{0:T(1024)}, u32[]{:S(2)}) copy-start(f32[1600]{0:T(1024)} %copy-done.28) | copy-start | bytes 19204
  749.1 84.2 %copy-start.31 = (f32[1600]{0:T(1024)S(1)}, f32[1600]{0:T(1024)}, u32[]{:S(2)}) copy-start(f32[1600]{0:T(1024)} %copy-done.30) | copy-start | bytes 19204
  749.1 84.2 %copy-start.34 = (f32[128]{0:T(128)S(1)}, f32[128]{0:T(128)}, u32[]{:S(2)}) copy-start(f32[128]{0:T(128)} %copy-done.33) | copy-start | bytes 1540
  749.1 84.2 %copy-start.36 = (f32[128]{0:T(128)S(1)}, f32[128]{0:T(128)}, u32[]{:S(2)}) copy-start(f32[128]{0:T(128)} %copy-done.35) | copy-start | bytes 1540
  749.1 546.8 %reduce-scatter.15.cloned.1.call-start = ((), (), s32[]{:S(2)}) async-start(), calls=%async_computation.16 | async-start | bytes 19456000 | tf_op jit(solution)/shard_map/reduce_scatter | solution.py:267
  750.5 91.3 %copy-start.21 = (bf16[128,25,64]{0,2,1:T(8,128)(2,1)}, bf16[128,25,64]{0,2,1:T(8,128)(2,1)S(1)}, u32[]{:S(2)}) copy-start(bf16[128,25,64]{0,2,1:T(8,128)(2,1)S(1)} %get-tuple-element.465) | copy-start | bytes 1228804
  781.9 59.9 %copy-start.22 = (bf16[128,1600]{0,1:T(8,128)(2,1)}, bf16[128,1600]{0,1:T(8,128)(2,1)S(1)}, u32[]{:S(2)}) copy-start(bf16[128,1600]{0,1:T(8,128)(2,1)S(1)} %copy.96) | copy-start | bytes 1228804
  833.3 8.5 copy-start.23
  849.6 201.4 %all-to-all-start.3 = ((bf16[4,400,1600]{2,1,0:T(8,128)(2,1)}), bf16[4,400,1600]{2,1,0:T(8,128)(2,1)}, u32[]{:S(2)}, u32[]{:S(2)}) async-start(bf16[4,400,1600]{2,1,0:T(8,128)(2,1)} %bitcast.213), calls=%async_computation.5 | async-start | bytes 10649600 | tf_op jit(solution)/shard_map/all_to_all | solution.py:178
  854.7 480.5 %reduce-scatter.19.cloned.1.call-start = ((), (), s32[]{:S(2)}) async-start(), calls=%async_computation.18 | async-start | bytes 2129920
  866.7 678.8 %all-reduce.16.cloned.1.call-start = ((), (), s32[]{:S(2)}) async-start(), calls=%async_computation.22 | async-start | bytes 31334400 | tf_op jit(solution)/shard_map/psum | solution.py:286
  1296.0 40.5 %copy-start.19 = (bf16[128,1600]{1,0:T(8,128)(2,1)S(1)}, bf16[128,1600]{1,0:T(8,128)(2,1)}, u32[]{:S(2)}) copy-start(bf16[128,1600]{1,0:T(8,128)(2,1)} %reduce-scatter.25.cloned.1.call-done) | copy-start | bytes 1228804
  1297.9 38.6 %all-to-all-start.2 = ((bf16[4,400,2]{1,2,0:T(2,128)(2,1)}), bf16[4,400,2]{1,2,0:T(2,128)(2,1)S(1)}, u32[]{:S(2)}, u32[]{:S(2)}) async-start(bf16[4,400,2]{1,2,0:T(2,128)(2,1)} %copy.83), calls=%async_computation.4 | async-start | bytes 16384 | tf_op jit(solution)/shard_map/all_to_all | solution.py:181
  1336.6 9.4 copy-start.50
  1336.6 27.3 %copy-start.38 = (bf16[1600]{0:T(1024)(128)(2,1)S(1)}, bf16[1600]{0:T(1024)(128)(2,1)}, u32[]{:S(2)}) copy-start(bf16[1600]{0:T(1024)(128)(2,1)} %get-tuple-element.460) | copy-start | bytes 9604
  1336.6 56.7 %copy-start.5 = (f32[128,1600]{0,1:T(8,128)S(1)}, f32[128,1600]{0,1:T(8,128)}, u32[]{:S(2)}) copy-start(f32[128,1600]{0,1:T(8,128)} %copy-done.4) | copy-start | bytes 2457604
  1336.6 56.7 %copy-start.9 = (bf16[128,1600]{0,1:T(8,128)(2,1)S(1)}, bf16[128,1600]{0,1:T(8,128)(2,1)}, u32[]{:S(2)}) copy-start(bf16[128,1600]{0,1:T(8,128)(2,1)} %copy.92) | copy-start | bytes 1228804
  1336.7 56.7 %copy-start.11 = (bf16[128,1600]{0,1:T(8,128)(2,1)S(1)}, bf16[128,1600]{0,1:T(8,128)(2,1)}, u32[]{:S(2)}) copy-start(bf16[128,1600]{0,1:T(8,128)(2,1)} %param.37) | copy-start | bytes 1228804
  1336.7 56.6 %copy-start.32 = (f32[1600]{0:T(1024)S(1)}, f32[1600]{0:T(1024)}, u32[]{:S(2)}) copy-start(f32[1600]{0:T(1024)} %get-tuple-element.378) | copy-start | bytes 19204
  1545.5 7.6 slice-start.2
  1545.5 6.0 copy-start.26
  1545.5 7.6 slice-start.3
  1551.5 6.4 slice-start
  (34 other events, 89.3 us)
Sparse Core Ops, SparseCore 0:
  9.6 269.6 all-gather.6
  292.8 31.6 all-gather.10
  326.9 33.2 all-gather.8
  361.7 164.0 all-gather.12
  527.2 37.6 all-gather.16
  566.9 36.9 all-gather.14
  627.2 35.6 reduce-scatter.20
  734.4 46.2 reduce-scatter.24
  784.7 47.3 reduce-scatter.22
  834.8 164.3 reduce-scatter.16
  1001.5 294.3 reduce-scatter.14
  1298.7 36.4 reduce-scatter.18
  1339.8 205.6 all-reduce.15
where the time goes:
time: 1580 us; the launch traced here: 1570 us
  waiting for transfers between devices  1150 us (73%)
  matrix products  151 us (10%)
  local copies, waits for them, and re-layouts  113 us (7%)
  blocking collectives  62.2 us (4%)
  other arithmetic  45.8 us (3%)
  starting transfers between devices  18.1 us (1%)
  between operations  16.5 us (1%)
    all_gather x1, waiting for transfers between devices, body(): lax.all_gather(qkv_weight, 'fsdp', axis=0, tiled=True)  247 us
    reduce_scatter x1, waiting for transfers between devices, body(): lax.psum_scatter(grad_qkv_w.astype(jnp.bfloat16), 'fsdp', scatter_dimensi...  228 us
    all_to_all x1, waiting for transfers between devices, body(): lax.all_to_all(grad_fc_cols.astype(jnp.bfloat16), 'fsdp', split_axis=0, c...  176 us
    unnamed x17, waiting for transfers between devices  152 us
    psum x1, waiting for transfers between devices, body(): lax.psum(owned_qkv.astype(jnp.bfloat16), 'ctx').astype(jnp.float32)  150 us
    all_gather x1, waiting for transfers between devices, body(): lax.all_gather(proj_weight, 'fsdp', axis=0, tiled=True)  129 us
    unnamed x127, local copies, waits for them, and re-layouts  40.2 us
    unnamed x2, blocking collectives  38 us
  transfers between devices with their start and end apart: 17, of which 13 were waited for; matrix products, arithmetic and copies ran while one was open for 10% of the time, Pallas kernels for 0%

commit v1 on v0

--- a/solution.py
+++ b/solution.py
@@ -1,3 +1,4 @@
+import functools
 import math
 import jax
 import jax.numpy as jnp
@@ -5,6 +6,30 @@
 from jax.sharding import PartitionSpec as P
 
 HEADS = 25
+
+
+def enter_cubes_up(local_block, along_axis):
+    q_n = lax.axis_size(along_axis)
+    row_list = []
+    for idx in range(q_n):
+        row_list.append((idx, (idx + 1) % q_n))
+    shelf = []
+    for idx in range(q_n):
+        shelf.append((idx, (idx - 1) % q_n))
+    upper, y_new = ([local_block], [local_block])
+    for _ in range(q_n // 2):
+        upper.append(lax.ppermute(upper[-1], along_axis, row_list))
+    for _ in range((q_n - 1) // 2):
+        y_new.append(lax.ppermute(y_new[-1], along_axis, shelf))
+    taken_in = jnp.roll(
+        jnp.concatenate([*upper[::-1], *y_new[1:]], axis=0),
+        shift=(lax.axis_index(along_axis) - q_n // 2) * local_block.shape[0],
+        axis=0,
+    )
+    return taken_in
+
+
+_enter_cubes = functools.partial(enter_cubes_up, along_axis="fsdp")
 
 
 def layer_norm(values, gain_vec, shift_vec):
@@ -55,7 +80,7 @@
         lax.all_gather(qkv_weight, "fsdp", axis=0, tiled=True),
         lax.all_gather(query_bias, "fsdp", axis=0, tiled=True),
         lax.all_gather(value_bias, "fsdp", axis=0, tiled=True),
-        lax.all_gather(proj_weight, "fsdp", axis=0, tiled=True),
+        _enter_cubes(proj_weight),
         lax.all_gather(proj_bias, "fsdp", axis=0, tiled=True),
     )
     inputs = tokens.astype(jnp.float32)

time: 1580 us -> 1530 us (0.968)
  waiting for transfers between devices: 1150 us -> 1090 us
    all_gather x1 -> x0, waiting for transfers between devices: 129 us -> none  [body(): lax.all_gather(proj_weight, 'fsdp', axis=0, tiled=True)]
    all_to_all x1, waiting for transfers between devices: 0.01 us -> 52.7 us  [body(): lax.all_to_all(small_tiled, 'fsdp', split_axis=1, concat_axis=0, tiled=True)]
    all_to_all x1, waiting for transfers between devices: 0.01 us -> 46.7 us  [body(): lax.all_to_all(fc_weight, 'fsdp', split_axis=1, concat_axis=0, tiled=True)]
    ppermute x0 -> x3, waiting for transfers between devices: none -> 32.9 us  [the longest x2 32.9 us: enter_cubes_up(): upper.append(lax.ppermute(upper[-1], along_axis, row_list))]
    all_gather x1, waiting for transfers between devices: 31.9 us -> 0.02 us  [body(): lax.all_gather(cotangent, 'fsdp', axis=0, tiled=True)]
    all_gather x1, waiting for transfers between devices: 31.1 us -> 0.01 us  [body(): lax.all_gather(normed_two, 'fsdp', axis=0, tiled=True)]
    unnamed x127 -> x134, local copies, waits for them, and re-layouts: 40.2 us -> 51.1 us
    unnamed x17 -> x16, waiting for transfers between devices: 152 us -> 151 us
  transfers between devices with their start and end apart: 17 -> 19, of which waited for: 13 -> 11; matrix products, arithmetic and copies ran while one was open for 10% -> 11% of each run, Pallas kernels for 0% -> 0%
where the time goes in v1:
time: 1530 us; the launch traced here: 1520 us
  waiting for transfers between devices  1090 us (71%)
  matrix products  155 us (10%)
  local copies, waits for them, and re-layouts  118 us (8%)
  blocking collectives  62.2 us (4%)
  other arithmetic  45.4 us (3%)
  starting transfers between devices  22 us (1%)
  between operations  16.8 us (1%)
    all_gather x1, waiting for transfers between devices, body(): lax.all_gather(qkv_weight, 'fsdp', axis=0, tiled=True)  247 us
    reduce_scatter x1, waiting for transfers between devices, body(): lax.psum_scatter(grad_qkv_w.astype(jnp.bfloat16), 'fsdp', scatter_dimensi...  228 us
    all_to_all x1, waiting for transfers between devices, body(): lax.all_to_all(grad_fc_cols.astype(jnp.bfloat16), 'fsdp', split_axis=0, c...  176 us
    unnamed x16, waiting for transfers between devices  151 us
    psum x1, waiting for transfers between devices, body(): lax.psum(owned_qkv.astype(jnp.bfloat16), 'ctx').astype(jnp.float32)  150 us
    all_to_all x1, waiting for transfers between devices, body(): lax.all_to_all(small_tiled, 'fsdp', split_axis=1, concat_axis=0, tiled=True)  52.7 us
    unnamed x134, local copies, waits for them, and re-layouts  51.1 us
    all_to_all x1, waiting for transfers between devices, body(): lax.all_to_all(fc_weight, 'fsdp', split_axis=1, concat_axis=0, tiled=True)  46.7 us
  transfers between devices with their start and end apart: 19, of which 11 were waited for; matrix products, arithmetic and copies ran while one was open for 11% of the time, Pallas kernels for 0%

profile of v1, /device:TPU:0, one launch (start us, length us, event | category | flops | bytes accessed | tf_op | source)
XLA Modules:
  0.0 1516.6 jit_solution(18275562951909616848)
XLA Ops:
  10.6 21.1 %all-reduce.13 = (bf16[1600]{0:T(1024)(128)(2,1)S(1)}, bf16[1600]{0:T(1024)(128)(2,1)S(1)}, bf16[1600]{0:T(1024)(128)(2,1)S(1)}, bf16[1600]{0:T(1024)(128)(2,1)S(1)}, bf16[1600]{0:T(1024)(128)(2,1)S(1)}) all-reduce(bf16[1600]{0:T(1024)(128)(2,1)S(1)} %dynamic-update-slice.2, ...), channel_id=1, replica_groups=mesh['ctx'=8,'fsdp'=4] {'fsdp'}, use_global_device_ids=true, to_apply=%add.2 | all-reduce | flops 8000 | bytes 32000
  32.3 247.1 %all-gather.6.cloned.1.call-done = bf16[1600,4800]{1,0:T(8,128)(2,1)} async-done(((bf16[400,4800]{1,0:T(8,128)(2,1)}), bf16[1600,4800]{1,0:T(8,128)(2,1)}) %all-gather.6.cloned.1.call-update) | async-done | bytes 15360016 | tf_op jit(solution)/shard_map/all_gather | solution.py:80
  279.4 12.1 fusion.80
  293.5 32.9 %collective-permute-done = bf16[400,1600]{1,0:T(8,128)(2,1)S(1)} collective-permute-done((bf16[400,1600]{1,0:T(8,128)(2,1)S(1)}, bf16[400,1600]{1,0:T(8,128)(2,1)S(1)}, u32[]{:S(2)}, u32[]{:S(2)}) %collective-permute-start) | collective-permute-done | bytes 1280032 | tf_op jit(solution)/shard_map/ppermute | solution.py:21
  335.2 11.7 all_to_all.51
  346.9 5.7 copy.78
  352.8 52.7 %all-to-all-done = bf16[400,4,3]{0,2,1:T(4,128)(2,1)S(1)} async-done(((bf16[400,4,3]{0,2,1:T(4,128)(2,1)}), bf16[400,4,3]{0,2,1:T(4,128)(2,1)S(1)}, u32[]{:S(2)}, u32[]{:S(2)}) %all-to-all-start) | async-done | bytes 9632 | tf_op jit(solution)/shard_map/all_to_all | solution.py:152
  405.6 5.1 all-to-all-start.1
  426.0 8.5 reshape.304
  437.1 19.6 %while.39 = (s32[]{:T(128)}, f32[25,128]{1,0:T(8,128)S(1)}, f32[25,128]{1,0:T(8,128)S(1)}, s32[2,512]{1,0:T(2,128)S(1)}, bf16[2,512,25,64]{1,3,2,0:T(8,128)(2,1)...) while((s32[]{:T(128)}, f32[25,128]{1,0:T(8,128)S(1)}, ...), condition=%wide.region_5.6_spmd.clone, body=%wide.region_2.5_spmd.clone.sunk | while | flops 221265664 | bytes 15526520 | solution.py:123
  437.5 5.2 fusion.187
  447.3 5.2 fusion.187
  456.7 8.5 reshape.303
  465.2 4.4 copy.75
  469.6 21.5 %while.40 = (s32[]{:T(128)}, f32[128,25,64]{0,2,1:T(8,128)}, bf16[2,512,25,64]{1,3,2,0:T(8,128)(2,1)}, s32[2,512]{1,0:T(2,128)S(1)}, bf16[2,512,25,64]{1,3,2,0:T...) while((s32[]{:T(128)}, f32[128,25,64]{0,2,1:T(8,128)}, ...), condition=%wide.region_7.8_spmd.clone, body=%wide.region_6.7_spmd.clone.sunk | while | flops 426459264 | bytes 5481595 | solution.py:135
  470.0 4.7 fusion.193
  475.0 5.0 fusion.193
  492.4 5.2 fusion.139
  499.8 7.9 fusion.140
  507.7 46.7 %all-to-all-done.1 = bf16[400,4,1600]{2,0,1:T(8,128)(2,1)} async-done(((bf16[400,4,1600]{2,0,1:T(8,128)(2,1)}), bf16[400,4,1600]{2,0,1:T(8,128)(2,1)}, u32[]{:S(2)}, u32[]{:S(2)}) %all-to-all-start.1) | async-done | bytes 5120032 | tf_op jit(solution)/shard_map/all_to_all | solution.py:151
  554.3 11.7 fusion.132
  567.2 6.7 convolution_convert_fusion.4
  577.6 35.7 %reduce-scatter.21.cloned.1.call-done = bf16[128,1600]{1,0:T(8,128)(2,1)} async-done(((bf16[512,1600]{1,0:T(8,128)(2,1)}), bf16[128,1600]{1,0:T(8,128)(2,1)}) %reduce-scatter.21.cloned.1.call-update) | async-done | bytes 409616
  620.7 4.3 fusion.98
  625.7 44.8 %while.41 = (s32[]{:T(128)}, f32[128,25,64]{0,2,1:T(8,128)}, bf16[2,512,25,64]{1,3,2,0:T(8,128)(2,1)}, bf16[2,512,25,64]{1,3,2,0:T(8,128)(2,1)}, bf16[2,512,25,6...) while((s32[]{:T(128)}, f32[128,25,64]{0,2,1:T(8,128)}, ...), condition=%wide.region_16.17_spmd.clone, body=%wide.region_15.16_spmd.clone.sunk | while | flops 1068712064 | bytes 98549520 | solution.py:256
  626.1 5.2 fusion.204
  631.7 6.4 fusion.205
  648.2 5.1 fusion.204
  653.6 6.4 fusion.205
  670.6 5.3 copy.81
  696.6 30.1 %reduce-scatter.23.cloned.1.call-done = bf16[128,1600]{1,0:T(8,128)(2,1)} async-done(((bf16[1024,1600]{1,0:T(8,128)(2,1)}), bf16[128,1600]{1,0:T(8,128)(2,1)}) %reduce-scatter.23.cloned.1.call-update) | async-done | bytes 409616
  728.0 50.1 %reduce-scatter.25.cloned.1.call-done = bf16[128,1600]{1,0:T(8,128)(2,1)} async-done(((bf16[1024,1600]{1,0:T(8,128)(2,1)}), bf16[128,1600]{1,0:T(8,128)(2,1)}) %reduce-scatter.25.cloned.1.call-update) | async-done | bytes 409616
  779.4 8.4 convolution_convert_fusion
  789.4 6.3 convolution_convert_fusion.2
  795.7 5.1 all-to-all-start.3
  801.1 8.0 convolution_convert_fusion.5
  812.8 8.1 convolution_convert_fusion.1
  821.0 176.4 %all-to-all-done.3 = bf16[4,400,1600]{2,1,0:T(8,128)(2,1)} async-done(((bf16[4,400,1600]{2,1,0:T(8,128)(2,1)}), bf16[4,400,1600]{2,1,0:T(8,128)(2,1)}, u32[]{:S(2)}, u32[]{:S(2)}) %all-to-all-start.3) | async-done | bytes 5120032 | tf_op jit(solution)/shard_map/all_to_all | solution.py:203
  997.4 6.9 copy.84
  1004.3 9.8 all_to_all.59
  1014.1 228.1 %reduce-scatter.15.cloned.1.call-done = bf16[400,4800]{1,0:T(8,128)(2,1)} async-done(((bf16[1600,4800]{1,0:T(8,128)(2,1)}), bf16[400,4800]{1,0:T(8,128)(2,1)}) %reduce-scatter.15.cloned.1.call-update) | async-done | bytes 3840016 | tf_op jit(solution)/shard_map/reduce_scatter | solution.py:292
  1248.0 33.6 %reduce-scatter.19.cloned.1.call-done = bf16[128,1600]{1,0:T(8,128)(2,1)} async-done(((bf16[512,1600]{1,0:T(8,128)(2,1)}), bf16[128,1600]{1,0:T(8,128)(2,1)}) %reduce-scatter.19.cloned.1.call-update) | async-done | bytes 409616
  1283.1 9.3 fusion.131
  1293.0 16.9 %all-reduce.12 = (bf16[1600]{0:T(1024)(128)(2,1)S(1)}, bf16[1600]{0:T(1024)(128)(2,1)S(1)}, bf16[1600]{0:T(1024)(128)(2,1)S(1)}, bf16[1600]{0:T(1024)(128)(2,1)S(1)}, bf16[1600]{0:T(1024)(128)(2,1)S(1)}) all-reduce(bf16[1600]{0:T(1024)(128)(2,1)S(1)} %get-tuple-element.374, ...), channel_id=6, replica_groups=mesh['ctx'=8,'fsdp'=4] {'fsdp'}, use_global_device_ids=true, to_apply=%region_22.23.clone | all-reduce | flops 8000 | bytes 32000
  1310.3 24.1 %all-reduce.10 = (bf16[400]{0:T(512)(128)(2,1)S(1)}, bf16[400]{0:T(512)(128)(2,1)S(1)}, bf16[400]{0:T(512)(128)(2,1)S(1)}, bf16[400]{0:T(512)(128)(2,1)S(1)}, bf...) all-reduce(bf16[400]{0:T(512)(128)(2,1)S(1)} %dynamic-slice.6, ...), channel_id=1, replica_groups=mesh['ctx'=8,'fsdp'=4] {'ctx'}, use_global_device_ids=true, to_apply=%region_23.24 | all-reduce | flops 4800 | bytes 19200 | tf_op jit(solution)/shard_map/psum | solution.py:309
  1341.7 150.1 %all-reduce.16.cloned.1.call-done = (bf16[400,4800]{1,0:T(8,128)(2,1)}, bf16[400,1600]{1,0:T(8,128)(2,1)}, bf16[400,6400]{1,0:T(8,128)(2,1)}, bf16[1600,1600]{1,0:T(8,128)(2,1)}) async-done(((bf16[400,4800]{1,0:T(8,128)(2,1)}, bf16[400,1600]{1,0:T(8,128)(2,1)}, bf16[400,6400]{1,0:T(8,128)(2,1)}, bf16[1600,1600]{1,0:T(8,128)(2,1)}), (bf16[400,4800]{1,0:T(8,128)(2,1)}, bf16[400,1600]{1,0:T(8,128)(2,1)}, ...) | async-done | bytes 15360016 | tf_op jit(solution)/shard_map/psum | solution.py:311
  1491.8 7.5 convert_element_type.281
  1499.3 4.7 convert_element_type.278
  (300 shorter events, 127.7 us)
Async XLA Ops:
  7.2 24.6 %copy-start.7 = (bf16[128,1600]{0,1:T(8,128)(2,1)S(1)}, bf16[128,1600]{0,1:T(8,128)(2,1)}, u32[]{:S(2)}) copy-start(bf16[128,1600]{0,1:T(8,128)(2,1)} %param.22) | copy-start | bytes 1228804
  7.3 272.1 %all-gather.6.cloned.1.call-start = ((), (), s32[]{:S(2)}) async-start(), calls=%async_computation.10 | async-start | bytes 19456000 | tf_op jit(solution)/shard_map/all_gather | solution.py:80
  8.0 418.0 %all-gather.10.cloned.1.call-start = ((), (), s32[]{:S(2)}) async-start(), calls=%async_computation.12 | async-start | bytes 3686400 | tf_op jit(solution)/shard_map/all_gather | solution.py:96
  31.8 247.6 %copy-start.28 = (f32[1600]{0:T(1024)}, f32[1600]{0:T(1024)S(1)}, u32[]{:S(2)}) copy-start(f32[1600]{0:T(1024)S(1)} %convert_element_type.230) | copy-start | bytes 19204
  31.8 247.6 %copy-start.30 = (f32[1600]{0:T(1024)}, f32[1600]{0:T(1024)S(1)}, u32[]{:S(2)}) copy-start(f32[1600]{0:T(1024)S(1)} %convert_element_type.231) | copy-start | bytes 19204
  32.1 247.3 %copy-start.33 = (f32[128]{0:T(128)}, f32[128]{0:T(128)S(1)}, u32[]{:S(2)}) copy-start(f32[128]{0:T(128)S(1)} %broadcast_multiply_fusion.2) | copy-start | bytes 1540
  32.3 247.1 %copy-start.49 = (f32[128]{0:T(128)}, f32[128]{0:T(128)S(1)}, u32[]{:S(2)}) copy-start(f32[128]{0:T(128)S(1)} %fusion.114) | copy-start | bytes 1540
  32.3 247.1 %copy-start.35 = (f32[128]{0:T(128)}, f32[128]{0:T(128)S(1)}, u32[]{:S(2)}) copy-start(f32[128]{0:T(128)S(1)} %fusion.124) | copy-start | bytes 1540
  291.6 38.7 %copy-start.41 = (bf16[400]{0:T(512)(128)(2,1)S(1)}, bf16[400]{0:T(512)(128)(2,1)}, u32[]{:S(2)}) copy-start(bf16[400]{0:T(512)(128)(2,1)} %param.31) | copy-start | bytes 2404
  291.6 38.7 %copy-start.42 = (bf16[400]{0:T(512)(128)(2,1)S(1)}, bf16[400]{0:T(512)(128)(2,1)}, u32[]{:S(2)}) copy-start(bf16[400]{0:T(512)(128)(2,1)} %param.32) | copy-start | bytes 2404
  291.6 38.7 %copy-start.43 = (bf16[400]{0:T(512)(128)(2,1)S(1)}, bf16[400]{0:T(512)(128)(2,1)}, u32[]{:S(2)}) copy-start(bf16[400]{0:T(512)(128)(2,1)} %param.36) | copy-start | bytes 2404
  291.6 43.2 %copy-start.39 = (s32[8,2]{0,1:T(2,128)S(1)}, s32[8,2]{0,1:T(2,128)}, u32[]{:S(2)}) copy-start(s32[8,2]{0,1:T(2,128)} %param.23) | copy-start | bytes 196
  292.7 164.0 %all-gather.8.cloned.1.call-start = ((), (), s32[]{:S(2)}) async-start(), calls=%async_computation.11 | async-start | bytes 3686400 | tf_op jit(solution)/shard_map/all_gather | solution.py:97
  293.5 33.0 %collective-permute-start = (bf16[400,1600]{1,0:T(8,128)(2,1)S(1)}, bf16[400,1600]{1,0:T(8,128)(2,1)S(1)}, u32[]{:S(2)}, u32[]{:S(2)}) collective-permute-start(bf16[400,1600]{1,0:T(8,128)(2,1)S(1)} %copy-done.12), channel_id=1, source_target_pairs={{0,1},{1,2},{2,3},{3,0},{4,5},{5,6},{6,7},{7,4},{8,9},{9,10},{10,1... | collective-permute-start | bytes 3840008 | tf_op jit(solution)/shard_map/ppermute | solution.py:21
  326.4 85.0 %collective-permute-start.1 = (bf16[400,1600]{1,0:T(8,128)(2,1)S(1)}, bf16[400,1600]{1,0:T(8,128)(2,1)}, u32[]{:S(2)}, u32[]{:S(2)}) collective-permute-start(bf16[400,1600]{1,0:T(8,128)(2,1)S(1)} %collective-permute-done), channel_id=1, source_target_pairs={{0,1},{1,2},{2,3},{3,0},{4,5},{5,6},{6,7},{7,4},{8,9},{9,10},{10,1... | collective-permute-start | bytes 3840008 | tf_op jit(solution)/shard_map/ppermute | solution.py:21
  326.4 89.8 %collective-permute-start.2 = (bf16[400,1600]{1,0:T(8,128)(2,1)S(1)}, bf16[400,1600]{1,0:T(8,128)(2,1)}, u32[]{:S(2)}, u32[]{:S(2)}) collective-permute-start(bf16[400,1600]{1,0:T(8,128)(2,1)S(1)} %copy-done.12), channel_id=1, source_target_pairs={{0,3},{1,0},{2,1},{3,2},{4,7},{5,4},{6,5},{7,6},{8,11},{9,8},{10,9... | collective-permute-start | bytes 3840008 | tf_op jit(solution)/shard_map/ppermute | solution.py:23
  330.9 74.6 %all-to-all-start = ((bf16[400,4,3]{0,2,1:T(4,128)(2,1)}), bf16[400,4,3]{0,2,1:T(4,128)(2,1)S(1)}, u32[]{:S(2)}, u32[]{:S(2)}) async-start(bf16[400,4,3]{0,2,1:T(4,128)(2,1)} %tile.2), calls=%async_computation | async-start | bytes 32768 | tf_op jit(solution)/shard_map/all_to_all | solution.py:152
  334.2 165.6 %all-gather.14.cloned.1.call-start = ((), (), s32[]{:S(2)}) async-start(), calls=%async_computation.14 | async-start | bytes 2048000 | tf_op jit(solution)/shard_map/all_gather | solution.py:160
  405.6 148.8 %all-to-all-start.1 = ((bf16[400,4,1600]{2,0,1:T(8,128)(2,1)}), bf16[400,4,1600]{2,0,1:T(8,128)(2,1)}, u32[]{:S(2)}, u32[]{:S(2)}) async-start(bf16[400,4,1600]{2,0,1:T(8,128)(2,1)} %copy.78), calls=%async_computation.1 | async-start | bytes 10649600 | tf_op jit(solution)/shard_map/all_to_all | solution.py:151
  410.6 143.7 %all-gather.12.cloned.1.call-start = ((), (), s32[]{:S(2)}) async-start(), calls=%async_computation.13 | async-start | bytes 2048000 | tf_op jit(solution)/shard_map/all_gather | solution.py:159
  492.3 7.4 copy-start.37
  499.7 113.5 %reduce-scatter.21.cloned.1.call-start = ((), (), s32[]{:S(2)}) async-start(), calls=%async_computation.18 | async-start | bytes 2129920
  577.5 149.2 %reduce-scatter.23.cloned.1.call-start = ((), (), s32[]{:S(2)}) async-start(), calls=%async_computation.19 | async-start | bytes 3833856
  631.6 6.5 copy-start.3
  653.6 6.5 copy-start.3
  680.3 97.8 %reduce-scatter.25.cloned.1.call-start = ((), (), s32[]{:S(2)}) async-start(), calls=%async_computation.20 | async-start | bytes 3833856
  690.0 324.1 %reduce-scatter.17.cloned.1.call-start = ((), (), s32[]{:S(2)}) async-start(), calls=%async_computation.16 | async-start | bytes 6656000 | tf_op jit(solution)/shard_map/reduce_scatter | solution.py:301
  695.1 84.2 %copy-start.8 = (bf16[128,1600]{0,1:T(8,128)(2,1)S(1)}, bf16[128,1600]{0,1:T(8,128)(2,1)}, u32[]{:S(2)}) copy-start(bf16[128,1600]{0,1:T(8,128)(2,1)} %param.22) | copy-start | bytes 1228804
  695.1 84.3 %copy-start.29 = (f32[1600]{0:T(1024)S(1)}, f32[1600]{0:T(1024)}, u32[]{:S(2)}) copy-start(f32[1600]{0:T(1024)} %copy-done.28) | copy-start | bytes 19204
  695.1 84.3 %copy-start.31 = (f32[1600]{0:T(1024)S(1)}, f32[1600]{0:T(1024)}, u32[]{:S(2)}) copy-start(f32[1600]{0:T(1024)} %copy-done.30) | copy-start | bytes 19204
  695.1 84.3 %copy-start.34 = (f32[128]{0:T(128)S(1)}, f32[128]{0:T(128)}, u32[]{:S(2)}) copy-start(f32[128]{0:T(128)} %copy-done.33) | copy-start | bytes 1540
  695.1 84.3 %copy-start.36 = (f32[128]{0:T(128)S(1)}, f32[128]{0:T(128)}, u32[]{:S(2)}) copy-start(f32[128]{0:T(128)} %copy-done.35) | copy-start | bytes 1540
  695.2 547.0 %reduce-scatter.15.cloned.1.call-start = ((), (), s32[]{:S(2)}) async-start(), calls=%async_computation.15 | async-start | bytes 19456000 | tf_op jit(solution)/shard_map/reduce_scatter | solution.py:292
  696.6 91.3 %copy-start.21 = (bf16[128,25,64]{0,2,1:T(8,128)(2,1)}, bf16[128,25,64]{0,2,1:T(8,128)(2,1)S(1)}, u32[]{:S(2)}) copy-start(bf16[128,25,64]{0,2,1:T(8,128)(2,1)S(1)} %get-tuple-element.465) | copy-start | bytes 1228804
  728.0 59.9 %copy-start.22 = (bf16[128,1600]{0,1:T(8,128)(2,1)}, bf16[128,1600]{0,1:T(8,128)(2,1)S(1)}, u32[]{:S(2)}) copy-start(bf16[128,1600]{0,1:T(8,128)(2,1)S(1)} %copy.94) | copy-start | bytes 1228804
  779.4 8.5 copy-start.23
  795.7 201.7 %all-to-all-start.3 = ((bf16[4,400,1600]{2,1,0:T(8,128)(2,1)}), bf16[4,400,1600]{2,1,0:T(8,128)(2,1)}, u32[]{:S(2)}, u32[]{:S(2)}) async-start(bf16[4,400,1600]{2,1,0:T(8,128)(2,1)} %bitcast.209), calls=%async_computation.5 | async-start | bytes 10649600 | tf_op jit(solution)/shard_map/all_to_all | solution.py:203
  800.8 480.8 %reduce-scatter.19.cloned.1.call-start = ((), (), s32[]{:S(2)}) async-start(), calls=%async_computation.17 | async-start | bytes 2129920
  812.8 679.0 %all-reduce.16.cloned.1.call-start = ((), (), s32[]{:S(2)}) async-start(), calls=%async_computation.21 | async-start | bytes 31334400 | tf_op jit(solution)/shard_map/psum | solution.py:311
  1242.2 40.7 %copy-start.19 = (bf16[128,1600]{1,0:T(8,128)(2,1)S(1)}, bf16[128,1600]{1,0:T(8,128)(2,1)}, u32[]{:S(2)}) copy-start(bf16[128,1600]{1,0:T(8,128)(2,1)} %reduce-scatter.25.cloned.1.call-done) | copy-start | bytes 1228804
  1244.0 38.8 %all-to-all-start.2 = ((bf16[4,400,2]{1,2,0:T(2,128)(2,1)}), bf16[4,400,2]{1,2,0:T(2,128)(2,1)S(1)}, u32[]{:S(2)}, u32[]{:S(2)}) async-start(bf16[4,400,2]{1,2,0:T(2,128)(2,1)} %copy.83), calls=%async_computation.4 | async-start | bytes 16384 | tf_op jit(solution)/shard_map/all_to_all | solution.py:206
  1283.0 9.4 copy-start.50
  1283.0 27.3 %copy-start.38 = (bf16[1600]{0:T(1024)(128)(2,1)S(1)}, bf16[1600]{0:T(1024)(128)(2,1)}, u32[]{:S(2)}) copy-start(bf16[1600]{0:T(1024)(128)(2,1)} %get-tuple-element.460) | copy-start | bytes 9604
  1283.0 56.7 %copy-start.5 = (f32[128,1600]{0,1:T(8,128)S(1)}, f32[128,1600]{0,1:T(8,128)}, u32[]{:S(2)}) copy-start(f32[128,1600]{0,1:T(8,128)} %copy-done.4) | copy-start | bytes 2457604
  1283.1 56.7 %copy-start.9 = (bf16[128,1600]{0,1:T(8,128)(2,1)S(1)}, bf16[128,1600]{0,1:T(8,128)(2,1)}, u32[]{:S(2)}) copy-start(bf16[128,1600]{0,1:T(8,128)(2,1)} %copy.92) | copy-start | bytes 1228804
  1283.1 56.7 %copy-start.15 = (bf16[128,1600]{0,1:T(8,128)(2,1)S(1)}, bf16[128,1600]{0,1:T(8,128)(2,1)}, u32[]{:S(2)}) copy-start(bf16[128,1600]{0,1:T(8,128)(2,1)} %param.37) | copy-start | bytes 1228804
  1283.1 56.6 %copy-start.32 = (f32[1600]{0:T(1024)S(1)}, f32[1600]{0:T(1024)}, u32[]{:S(2)}) copy-start(f32[1600]{0:T(1024)} %get-tuple-element.378) | copy-start | bytes 19204
  1491.8 7.5 copy-start.13
  (28 other events, 78.5 us)
Sparse Core Ops, SparseCore 0:
  9.6 269.7 all-gather.5
  292.8 31.5 all-gather.9
  326.9 33.2 all-gather.7
  361.6 83.6 all-gather.13
  499.8 52.6 all-gather.11
  577.6 35.5 reduce-scatter.20
  680.4 46.2 reduce-scatter.22
  730.7 47.3 reduce-scatter.24
  781.0 164.4 reduce-scatter.16
  947.7 294.4 reduce-scatter.14
  1245.1 36.4 reduce-scatter.18
  1286.1 205.6 all-reduce.15
